TPU v7x, 32 devices: a whole 2x2x4 slice. The times are simulated.
32 devices in a mesh: dp: 8 (over y, x, core), mp: 4 (over z).
Axes of the slice: x: 2, y: 2, z: 4, core: 2. Of those that a mesh axis runs over, the one named last changes fastest.
Arguments:
- tokens: bfloat16 [4096, 1024], P('dp', 'mp'), may hold values from -150 to 150
- pre_gain: bfloat16 [1024], P('mp'), may hold values from 0.25 to 1.75
- input_weight: bfloat16 [3, 1024, 1024], P(None, 'dp', 'mp'), may hold values from -0.125 to 0.125
- output_weight: bfloat16 [1024, 1024], P('mp', 'dp'), may hold values from -1 to 1
- position_bias: bfloat16 [16, 512, 512], P('mp'), may hold values from -3 to 353
- post_gain: bfloat16 [1024], P('mp'), may hold values from 0.25 to 1.75
Outputs:
- stream: bfloat16 [4096, 1024], P('dp', 'mp')
- normed: bfloat16 [4096, 1024], P('dp', 'mp')
All inputs are finite; a program needn't handle non-finite values.
Results may differ from a plain program's by a relative error of at most 0.013.
Values may be sent and summed in bfloat16 or wider, within the bound.
A program may use at most 64 MiB of HBM per device.

v0:
```python
import jax
import jax.numpy as jnp
from jax import lax
from jax.sharding import PartitionSpec as P

epsilon = 1e-06


def attend_all(mixed_heads, position_bias):
    row_count = mixed_heads.shape[1]
    inner_width = mixed_heads.shape[2]
    head_count = position_bias.shape[0]
    seq_len = position_bias.shape[1]
    grouped = mixed_heads.reshape(
        3, row_count // seq_len, seq_len, head_count, inner_width // head_count
    )
    bias_wide = position_bias.astype(jnp.float32)

    def one_sequence(sequence):
        sequence_block = lax.dynamic_index_in_dim(grouped, sequence, 1, keepdims=False)
        scores = (
            jnp.einsum(
                "qhd,khd->hqk",
                sequence_block[0],
                sequence_block[1],
                preferred_element_type=jnp.float32,
            )
            + bias_wide
        )
        row_max = jnp.max(scores, axis=2, keepdims=True)
        weights = jnp.exp(scores - row_max)
        probabilities = (weights / jnp.sum(weights, axis=2, keepdims=True)).astype(jnp.bfloat16)
        context = jnp.einsum(
            "hqk,khd->qhd", probabilities, sequence_block[2], preferred_element_type=jnp.float32
        )
        return context.reshape(seq_len, inner_width).astype(jnp.bfloat16)

    stacked = lax.map(one_sequence, jnp.arange(row_count // seq_len, dtype=jnp.int32))
    return stacked.reshape(row_count, inner_width)


def on_device(tokens, pre_gain, input_weight, output_weight, position_bias, post_gain):
    rows_all, gain_all = (
        lax.all_gather(tokens, "mp", axis=1, tiled=True),
        lax.all_gather(pre_gain, "mp", axis=0, tiled=True),
    )
    widened = rows_all.astype(jnp.float32)
    inverse_rms = lax.rsqrt(jnp.mean(widened * widened, axis=1, keepdims=True) + epsilon)
    normed_in = (widened * inverse_rms * gain_all.astype(jnp.float32)).astype(jnp.bfloat16)
    feature_count = tokens.shape[1]
    projected = jnp.einsum(
        "td,kdi->kti",
        normed_in,
        lax.all_gather(input_weight, "dp", axis=1, tiled=True),
        preferred_element_type=jnp.float32,
    )
    context = attend_all(projected.astype(jnp.bfloat16), position_bias)
    partial_value = jnp.dot(
        context,
        lax.all_gather(output_weight, "dp", axis=1, tiled=True),
        preferred_element_type=jnp.float32,
    )
    attention_out = lax.psum_scatter(
        partial_value.astype(jnp.bfloat16), "mp", scatter_dimension=1, tiled=True
    ).astype(jnp.float32)
    stream = (tokens.astype(jnp.float32) + attention_out).astype(jnp.bfloat16)
    restored = lax.optimization_barrier(stream).astype(jnp.float32)
    squares = lax.psum(jnp.sum(restored * restored, axis=1), "mp")
    post_rms = lax.rsqrt(squares[:, None] / (feature_count * lax.axis_size("mp")) + epsilon)
    normed = (restored * post_rms * post_gain.astype(jnp.float32)).astype(jnp.bfloat16)
    return (stream, normed)


def solution(mesh):
    return jax.shard_map(
        on_device,
        mesh=mesh,
        in_specs=(
            P("dp", "mp"),
            P("mp"),
            P(None, "dp", "mp"),
            P("mp", "dp"),
            P("mp", None, None),
            P("mp"),
        ),
        out_specs=(P("dp", "mp"), P("dp", "mp")),
        check_vma=False,
    )
```

profile of v0, /device:TPU:0, one launch (start us, length us, event | category | flops | bytes accessed | tf_op | source)
XLA Modules:
  0.0 123.4 jit_solution(2190378064825369234)
XLA Ops:
  7.2 0.0 all-gather.4.cloned.1.call-start
  7.2 0.7 all-gather.4.cloned.1.call-update
  7.9 0.0 all-gather.6.cloned.1.call-start
  7.9 1.7 %copy.11 = bf16[3,128,256]{1,2,0:T(8,128)(2,1)} copy(bf16[3,128,256]{2,1,0:T(8,128)(2,1)} %param.8) | data formatting | bytes 393216 | tf_op args[2]
  9.7 0.0 all-gather.6.cloned.1.call-update
  9.7 0.0 reduce-scatter.2.cloned.1.call-start
  9.8 0.7 reshape.34
  10.4 12.6 %all-gather = bf16[4,1,256]{2,1,0:T(2,128)(2,1)S(1)} all-gather(bf16[1,1,256]{2,1,0:T(2,128)(2,1)S(1)} %reshape.34), channel_id=1, replica_groups=mesh['dp'=8,'mp'=4] {'mp'}, dimensions={0}, use_global_device_ids=true | all-gather | bytes 2560 | tf_op jit(solution)/shard_map/all_gather | solution.py:45
  23.1 0.0 copy-start.2
  23.1 2.8 %copy.12 = bf16[4,512,512]{1,2,0:T(8,128)(2,1)S(1)} copy(bf16[4,512,512]{2,1,0:T(8,128)(2,1)} %param.10) | data formatting | bytes 4194304 | tf_op args[4]
  25.9 0.0 copy-done.2
  25.9 10.0 %all_gather.15 = bf16[256,1024]{1,0:T(8,128)(2,1)S(1)} all-gather(bf16[256,128]{1,0:T(8,128)(2,1)S(1)} %copy-done.2), channel_id=1, replica_groups=mesh['dp'=8,'mp'=4] {'dp'}, dimensions={1}, use_global_device_ids=true | all-gather | bytes 589824 | tf_op jit(solution)/shard_map/all_gather | solution.py:60
  35.9 6.2 %all-gather.4.cloned.1.call-done = bf16[512,1024]{1,0:T(8,128)(2,1)} async-done(((bf16[512,256]{1,0:T(8,128)(2,1)}), bf16[512,1024]{1,0:T(8,128)(2,1)}) %all-gather.4.cloned.1.call-update) | async-done | bytes 1048592 | tf_op jit(solution)/shard_map/all_gather | solution.py:44
  42.1 1.5 %fusion.2 = f32[512]{0:T(512)S(1)} fusion(bf16[512,1024]{1,0:T(8,128)(2,1)} %all-gather.4.cloned.1.call-done), kind=kLoop, calls=%fused_computation.7 | loop fusion | flops 1572352 | bytes 1050624 | tf_op jit(solution)/shard_map/reduce_sum | solution.py:48
  43.6 25.1 %all-gather.6.cloned.1.call-done = bf16[3,1024,256]{1,2,0:T(8,128)(2,1)} async-done(((bf16[3,128,256]{1,2,0:T(8,128)(2,1)}), bf16[3,1024,256]{1,2,0:T(8,128)(2,1)}) %all-gather.6.cloned.1.call-update) | async-done | bytes 1572880 | tf_op jit(solution)/shard_map/all_gather | solution.py:54
  68.7 2.8 %fusion.6 = bf16[3,512,256]{1,2,0:T(8,128)(2,1)S(1)} fusion(bf16[3,1024,256]{1,2,0:T(8,128)(2,1)} %all-gather.6.cloned.1.call-done, bf16[512,1024]{1,0:T(8,128)(2,1)} %all-gather.4.cloned.1.call-done, f32[1024]{0:T(1024)S(1)} %bitcast.26, f32[512]{0:T(512)S(1)} %add_rsqrt_fusion.1), kind=kOutput, calls=%fused_computation.13 | convolution fusion | flops 807796736 | bytes 3414016 | tf_op jit(solution)/shard_map/td,kdi->kti/dot_general | solution.py:51
  71.5 0.8 fusion.18
  72.3 1.5 %fusion.19 = f32[4,512]{1,0:T(4,128)S(1)} fusion(bf16[4,512,512]{1,2,0:T(8,128)(2,1)S(1)} %copy.12, bf16[512,4,64]{0,2,1:T(8,128)(2,1)S(1)} %bitcast.23, bf16[512,4,64]{0,2,1:T(8,128)(2,1)S(1)} %bitcast.21), kind=kOutput, calls=%fused_computation.29 | convolution fusion | flops 138412544 | bytes 2629632 | tf_op jit(solution)/shard_map/while/body/eval_jaxpr/sub | solution.py:31
  73.8 2.9 %fusion.7 = bf16[4,64,512]{2,1,0:T(8,128)(2,1)S(1)} fusion(bf16[512,4,64]{0,2,1:T(8,128)(2,1)} %bitcast.25, f32[4,512]{1,0:T(4,128)S(1)} %fusion.19, bf16[4,512,512]{1,2,0:T(8,128)(2,1)S(1)} %copy.12, bf16[512,4,64]{0,2,1:T(8,128)(2,1)S(1)} %bitcast.24, bf16[512,4,64]{0,2,1:T(8,128)(2,1)S(1)} %bitcast.22), kind=kOutput, calls=%fused_computation.14 | convolution fusion | flops 273811968 | bytes 3153920 | tf_op jit(solution)/shard_map/while/body/eval_jaxpr/hqk,khd->qhd/dot_general | solution.py:33
  76.6 0.0 copy-start.3
  76.6 0.0 copy-start.1
  76.6 1.4 %convolution_convert_fusion = bf16[512,1024]{1,0:T(8,128)(2,1)} fusion(bf16[512,256]{0,1:T(8,128)(2,1)S(1)} %bitcast.20, bf16[256,1024]{1,0:T(8,128)(2,1)S(1)} %all_gather.15), kind=kOutput, calls=%fused_computation.11 | convolution fusion | flops 268959744 | bytes 1835008 | tf_op jit(solution)/shard_map/dot_general | solution.py:58
  78.1 0.0 reduce-scatter.2.cloned.1.call-update
  78.1 0.0 copy-done.3
  78.1 27.4 %reduce-scatter.2.cloned.1.call-done = bf16[512,256]{1,0:T(8,128)(2,1)} async-done(((bf16[512,1024]{1,0:T(8,128)(2,1)}), bf16[512,256]{1,0:T(8,128)(2,1)}) %reduce-scatter.2.cloned.1.call-update) | async-done | bytes 262160 | tf_op jit(solution)/shard_map/reduce_scatter | solution.py:63
  105.6 0.0 copy-done.1
  105.6 1.0 add_convert_fusion
  106.6 0.0 copy-start
  106.6 0.1 fusion.12
  106.7 9.3 %psum.7 = f32[512]{0:T(512)S(1)} all-reduce(f32[512]{0:T(512)S(1)} %fusion.12), channel_id=1, replica_groups=mesh['dp'=8,'mp'=4] {'mp'}, use_global_device_ids=true, to_apply=%region_5.6 | all-reduce | flops 512 | bytes 4096 | tf_op jit(solution)/shard_map/psum | solution.py:68
  116.0 0.8 fusion.14
  116.9 0.0 copy-done
  (4 shorter events, 0.0 us)
Async XLA Ops:
  7.2 35.0 %all-gather.4.cloned.1.call-start = ((), (), s32[]{:S(2)}) async-start(), calls=%async_computation.1 | async-start | bytes 1310720 | tf_op jit(solution)/shard_map/all_gather | solution.py:44
  7.9 60.8 %all-gather.6.cloned.1.call-start = ((), (), s32[]{:S(2)}) async-start(), calls=%async_computation.2 | async-start | bytes 1769472 | tf_op jit(solution)/shard_map/all_gather | solution.py:54
  9.7 95.8 %reduce-scatter.2.cloned.1.call-start = ((), (), s32[]{:S(2)}) async-start(), calls=%async_computation.3 | async-start | bytes 1310720 | tf_op jit(solution)/shard_map/reduce_scatter | solution.py:63
  23.1 2.8 %copy-start.2 = (bf16[256,128]{1,0:T(8,128)(2,1)S(1)}, bf16[256,128]{1,0:T(8,128)(2,1)}, u32[]{:S(2)}) copy-start(bf16[256,128]{1,0:T(8,128)(2,1)} %param.9) | copy-start | bytes 196612
  76.6 1.5 %copy-start.3 = (bf16[256]{0:T(256)(128)(2,1)S(1)}, bf16[256]{0:T(256)(128)(2,1)}, u32[]{:S(2)}) copy-start(bf16[256]{0:T(256)(128)(2,1)} %param.11) | copy-start | bytes 1540
  76.6 28.9 %copy-start.1 = (bf16[512,256]{1,0:T(8,128)(2,1)S(1)}, bf16[512,256]{1,0:T(8,128)(2,1)}, u32[]{:S(2)}) copy-start(bf16[512,256]{1,0:T(8,128)(2,1)} %param.6) | copy-start | bytes 786436
  106.6 10.3 %copy-start = (bf16[512,256]{1,0:T(8,128)(2,1)}, bf16[512,256]{1,0:T(8,128)(2,1)S(1)}, u32[]{:S(2)}) copy-start(bf16[512,256]{1,0:T(8,128)(2,1)S(1)} %add_convert_fusion) | copy-start | bytes 786436
Sparse Core Ops, SparseCore 0:
  9.5 32.5 all-gather.3
  44.6 24.0 all-gather.5
  78.2 27.2 reduce-scatter.1
where the time goes:
time: 124 us; the launch traced here: 123 us
  waiting for transfers between devices  59.4 us (48%)
  blocking collectives  31.9 us (26%)
  between operations  13.8 us (11%)
  matrix products  8.6 us (7%)
  local copies, waits for them, and re-layouts  6 us (5%)
  other arithmetic  3.54 us (3%)
    reduce_scatter x1, waiting for transfers between devices, on_device(): lax.psum_scatter(partial_value.astype(jnp.bfloat16), 'mp', scatter_dimens...  27.4 us
    all_gather x1, waiting for transfers between devices, on_device(): lax.all_gather(input_weight, 'dp', axis=1, tiled=True)  25.1 us
    all_gather x1, blocking collectives, on_device(): lax.all_gather(pre_gain, 'mp', axis=0, tiled=True)  12.6 us
    all_gather x1, blocking collectives, on_device(): lax.all_gather(output_weight, 'dp', axis=1, tiled=True)  9.99 us
    psum x1, blocking collectives, on_device(): squares = lax.psum(jnp.sum(restored * restored, axis=1), 'mp')  9.28 us
    all_gather x1, waiting for transfers between devices, on_device(): lax.all_gather(tokens, 'mp', axis=1, tiled=True)  6.23 us
    unnamed x11, local copies, waits for them, and re-layouts  5.24 us
    dot_general x1, matrix products, one_sequence(): jnp.einsum('hqk,khd->qhd', probabilities, sequence_block[2], preferred_el...  2.86 us
  transfers between devices with their start and end apart: 3, of which 3 were waited for; matrix products, arithmetic and copies ran while one was open for 5% of the time, Pallas kernels for 0%

commit v1 on v0

--- a/solution.py
+++ b/solution.py
@@ -4,6 +4,24 @@
 from jax.sharding import PartitionSpec as P
 
 epsilon = 1e-06
+
+
+def ring_gather(array, axis, dim):
+    ways, here, step = (lax.axis_size(axis), lax.axis_index(axis), array.shape[dim])
+    dims = [n * ways if d == dim else n for d, n in enumerate(array.shape)]
+    full = lax.dynamic_update_slice_in_dim(
+        jnp.zeros(dims, array.dtype), array, here * step, axis=dim
+    )
+    going_up = going_down = array
+    for far in range(1, ways // 2 + 1):
+        going_up = lax.ppermute(going_up, axis, [(d, (d + 1) % ways) for d in range(ways)])
+        full = lax.dynamic_update_slice_in_dim(full, going_up, (here - far) % ways * step, axis=dim)
+        if 2 * far < ways:
+            going_down = lax.ppermute(going_down, axis, [(d, (d - 1) % ways) for d in range(ways)])
+            full = lax.dynamic_update_slice_in_dim(
+                full, going_down, (here + far) % ways * step, axis=dim
+            )
+    return full
 
 
 def attend_all(mixed_heads, position_bias):
@@ -51,7 +69,7 @@
     projected = jnp.einsum(
         "td,kdi->kti",
         normed_in,
-        lax.all_gather(input_weight, "dp", axis=1, tiled=True),
+        ring_gather(input_weight, "dp", 1),
         preferred_element_type=jnp.float32,
     )
     context = attend_all(projected.astype(jnp.bfloat16), position_bias)

time: 124 us -> 118 us (0.952)
  waiting for transfers between devices: 59.4 us -> 34.8 us
  local copies, waits for them, and re-layouts: 6 us -> 16.3 us
  starting transfers between devices: 0.12 us -> 9.1 us
    all_gather x1 -> x0, waiting for transfers between devices: 25.1 us -> none  [on_device(): lax.all_gather(input_weight, 'dp', axis=1, tiled=True)]
    ppermute x0 -> x7, waiting for transfers between devices: none -> 10.1 us  [the longest x4 9.31 us: ring_gather(): lax.ppermute(going_up, axis, [(d, (d + 1) % ways) for d in range(ways)])]
    ppermute x0 -> x7, starting transfers between devices: none -> 9.02 us  [the longest x3 7.9 us: ring_gather(): lax.ppermute(going_down, axis, [(d, (d - 1) % ways) for d in range(ways)])]
    all_gather x1, waiting for transfers between devices: 6.23 us -> 0.01 us  [on_device(): lax.all_gather(tokens, 'mp', axis=1, tiled=True)]
    dynamic_update_slice x0 -> x8, local copies, waits for them, and re-layouts: none -> 5.71 us  [the longest x4 2.86 us: ring_gather(): lax.dynamic_update_slice_in_dim(full, going_up, (here - far) % ways * ste...]
    ppermute x0 -> x7, local copies, waits for them, and re-layouts: none -> 3.9 us  [the longest x4 2.49 us: ring_gather(): lax.ppermute(going_up, axis, [(d, (d + 1) % ways) for d in range(ways)])]
    reduce_scatter x1, waiting for transfers between devices: 27.4 us -> 23.9 us  [on_device(): lax.psum_scatter(partial_value.astype(jnp.bfloat16), 'mp', scatter_dimens...]
    broadcast_in_dim x0 -> x1, local copies, waits for them, and re-layouts: none -> 1.35 us  [ring_gather(): jnp.zeros(dims, array.dtype)]
  transfers between devices with their start and end apart: 3 -> 9, of which waited for: 3 -> 5; matrix products, arithmetic and copies ran while one was open for 5% -> 13% of each run, Pallas kernels for 0% -> 0%
where the time goes in v1:
time: 118 us
  waiting for transfers between devices  34.8 us (29%)
  blocking collectives  31.2 us (26%)
  local copies, waits for them, and re-layouts  16.3 us (14%)
  between operations  14.3 us (12%)
  starting transfers between devices  9.1 us (8%)
  matrix products  8.64 us (7%)
  other arithmetic  3.54 us (3%)
    reduce_scatter x1, waiting for transfers between devices, on_device(): lax.psum_scatter(partial_value.astype(jnp.bfloat16), 'mp', scatter_dimens...  23.9 us
    all_gather x1, blocking collectives, on_device(): lax.all_gather(pre_gain, 'mp', axis=0, tiled=True)  12 us
    all_gather x1, blocking collectives, on_device(): lax.all_gather(output_weight, 'dp', axis=1, tiled=True)  9.99 us
    ppermute x4, waiting for transfers between devices, ring_gather(): lax.ppermute(going_up, axis, [(d, (d + 1) % ways) for d in range(ways)])  9.31 us
    psum x1, blocking collectives, on_device(): squares = lax.psum(jnp.sum(restored * restored, axis=1), 'mp')  9.27 us
    ppermute x3, starting transfers between devices, ring_gather(): lax.ppermute(going_down, axis, [(d, (d - 1) % ways) for d in range(ways)])  7.9 us
    unnamed x13, local copies, waits for them, and re-layouts  4.63 us
    dot_general x1, matrix products, one_sequence(): jnp.einsum('hqk,khd->qhd', probabilities, sequence_block[2], preferred_el...  2.93 us
  transfers between devices with their start and end apart: 9, of which 5 were waited for; matrix products, arithmetic and copies ran while one was open for 13% of the time, Pallas kernels for 0%

profile of v1, /device:TPU:0, one launch (start us, length us, event | category | flops | bytes accessed | tf_op | source)
XLA Modules:
  0.0 118.0 jit_solution(18387594913993419635)
XLA Ops:
  8.5 2.9 %collective-permute-start.1 = (bf16[3,128,256]{2,1,0:T(8,128)(2,1)}, bf16[3,128,256]{2,1,0:T(8,128)(2,1)S(1)}, u32[]{:S(2)}, u32[]{:S(2)}) collective-permute-start(bf16[3,128,256]{2,1,0:T(8,128)(2,1)} %param.8), channel_id=1, source_target_pairs={{0,28},{4,0},{8,4},{12,8},{16,12},{20,16},{24,20},{28,24},{1,29},{... | collective-permute-start | bytes 589832 | tf_op jit(solution)/shard_map/ppermute | solution.py:20
  11.4 1.1 copy.18
  13.3 12.0 %all-gather = bf16[4,1,256]{2,1,0:T(2,128)(2,1)S(1)} all-gather(bf16[1,1,256]{2,1,0:T(2,128)(2,1)S(1)} %reshape.34), channel_id=1, replica_groups=mesh['dp'=8,'mp'=4] {'mp'}, dimensions={0}, use_global_device_ids=true | all-gather | bytes 2560 | tf_op jit(solution)/shard_map/all_gather | solution.py:63
  25.3 2.8 %copy.26 = bf16[4,512,512]{1,2,0:T(8,128)(2,1)S(1)} copy(bf16[4,512,512]{2,1,0:T(8,128)(2,1)} %param.10) | data formatting | bytes 4194304 | tf_op args[4]
  28.2 10.0 %all_gather.11 = bf16[256,1024]{1,0:T(8,128)(2,1)S(1)} all-gather(bf16[256,128]{1,0:T(8,128)(2,1)S(1)} %copy-done.3), channel_id=1, replica_groups=mesh['dp'=8,'mp'=4] {'dp'}, dimensions={1}, use_global_device_ids=true | all-gather | bytes 589824 | tf_op jit(solution)/shard_map/all_gather | solution.py:78
  38.2 1.3 %broadcast_in_dim.6 = bf16[3,1024,256]{1,2,0:T(8,128)(2,1)} broadcast(bf16[]{:T(256)} %constant.72.clone.1), dimensions={} | broadcast | bytes 1572866 | tf_op jit(solution)/shard_map/broadcast_in_dim | solution.py:13
  41.0 2.3 %collective-permute-start.3 = (bf16[3,128,256]{2,1,0:T(8,128)(2,1)S(1)}, bf16[3,128,256]{2,1,0:T(8,128)(2,1)}, u32[]{:S(2)}, u32[]{:S(2)}) collective-permute-start(bf16[3,128,256]{2,1,0:T(8,128)(2,1)S(1)} %collective-permute-done.1), channel_id=1, source_target_pairs={{0,28},{4,0},{8,4},{12,8},{16,12},{20,16},{24,20},{28,24},{1,29},{... | collective-permute-start | bytes 589832 | tf_op jit(solution)/shard_map/ppermute | solution.py:20
  43.3 0.7 constant_dynamic-update-slice_fusion.6
  44.0 0.7 constant_dynamic-update-slice_fusion.5
  44.7 2.8 %collective-permute-done.2 = bf16[3,128,256]{2,1,0:T(8,128)(2,1)} collective-permute-done((bf16[3,128,256]{2,1,0:T(8,128)(2,1)S(1)}, bf16[3,128,256]{2,1,0:T(8,128)(2,1)}, u32[]{:S(2)}, u32[]{:S(2)}) %collective-permute-start.2) | collective-permute-done | bytes 196640 | tf_op jit(solution)/shard_map/ppermute | solution.py:17
  47.5 1.1 copy.21
  48.7 1.1 copy.22
  49.8 2.7 %collective-permute-start.5 = (bf16[3,128,256]{2,1,0:T(8,128)(2,1)}, bf16[3,128,256]{2,1,0:T(8,128)(2,1)S(1)}, u32[]{:S(2)}, u32[]{:S(2)}) collective-permute-start(bf16[3,128,256]{2,1,0:T(8,128)(2,1)} %collective-permute-done.3), channel_id=1, source_target_pairs={{0,28},{4,0},{8,4},{12,8},{16,12},{20,16},{24,20},{28,24},{1,29},{... | collective-permute-start | bytes 589832 | tf_op jit(solution)/shard_map/ppermute | solution.py:20
  52.4 0.7 constant_dynamic-update-slice_fusion.4
  53.2 0.7 constant_dynamic-update-slice_fusion.3
  53.9 2.9 %collective-permute-done.4 = bf16[3,128,256]{2,1,0:T(8,128)(2,1)S(1)} collective-permute-done((bf16[3,128,256]{2,1,0:T(8,128)(2,1)}, bf16[3,128,256]{2,1,0:T(8,128)(2,1)S(1)}, u32[]{:S(2)}, u32[]{:S(2)}) %collective-permute-start.4) | collective-permute-done | bytes 196640 | tf_op jit(solution)/shard_map/ppermute | solution.py:17
  57.0 0.8 collective-permute-done.5
  57.9 0.7 constant_dynamic-update-slice_fusion.2
  58.7 0.7 constant_dynamic-update-slice_fusion.1
  59.4 3.6 %collective-permute-done.6 = bf16[3,128,256]{2,1,0:T(8,128)(2,1)} collective-permute-done((bf16[3,128,256]{2,1,0:T(8,128)(2,1)S(1)}, bf16[3,128,256]{2,1,0:T(8,128)(2,1)}, u32[]{:S(2)}, u32[]{:S(2)}) %collective-permute-start.6) | collective-permute-done | bytes 196640 | tf_op jit(solution)/shard_map/ppermute | solution.py:17
  63.0 1.1 copy.25
  64.1 0.7 constant_dynamic-update-slice_fusion
  64.9 1.5 %fusion.2 = f32[512]{0:T(512)S(1)} fusion(bf16[512,1024]{1,0:T(8,128)(2,1)} %all-gather.3.cloned.1.call-done), kind=kLoop, calls=%fused_computation.7 | loop fusion | flops 1572352 | bytes 1050624 | tf_op jit(solution)/shard_map/reduce_sum | solution.py:66
  66.4 2.8 %fusion.6 = bf16[3,512,256]{1,2,0:T(8,128)(2,1)S(1)} fusion(bf16[3,1024,256]{1,2,0:T(8,128)(2,1)} %constant_dynamic-update-slice_fusion, bf16[512,1024]{1,0:T(8,128)(2,1)} %all-gather.3.cloned.1.call-done, f32[1024]{0:T(1024)S(1)} %bitcast.26, f32[512]{0:T(512)S(1)} %add_rsqrt_fusion.1), kind=kOutput, calls=%fused_computation.13 | convolution fusion | flops 807796736 | bytes 3414016 | tf_op jit(solution)/shard_map/td,kdi->kti/dot_general | solution.py:69
  69.2 0.8 fusion.18
  69.9 1.5 %fusion.19 = f32[4,512]{1,0:T(4,128)S(1)} fusion(bf16[4,512,512]{1,2,0:T(8,128)(2,1)S(1)} %copy.26, bf16[512,4,64]{0,2,1:T(8,128)(2,1)S(1)} %bitcast.23, bf16[512,4,64]{0,2,1:T(8,128)(2,1)S(1)} %bitcast.21), kind=kOutput, calls=%fused_computation.37 | convolution fusion | flops 138412544 | bytes 2629632 | tf_op jit(solution)/shard_map/while/body/eval_jaxpr/sub | solution.py:49
  71.4 2.9 %fusion.7 = bf16[4,64,512]{2,1,0:T(8,128)(2,1)S(1)} fusion(bf16[512,4,64]{0,2,1:T(8,128)(2,1)} %bitcast.25, f32[4,512]{1,0:T(4,128)S(1)} %fusion.19, bf16[4,512,512]{1,2,0:T(8,128)(2,1)S(1)} %copy.26, bf16[512,4,64]{0,2,1:T(8,128)(2,1)} %bitcast.24, bf16[512,4,64]{0,2,1:T(8,128)(2,1)S(1)} %bitcast.22), kind=kOutput, calls=%fused_computation.14 | convolution fusion | flops 273811968 | bytes 3153920 | tf_op jit(solution)/shard_map/while/body/eval_jaxpr/hqk,khd->qhd/dot_general | solution.py:51
  74.4 1.4 %convolution_convert_fusion = bf16[512,1024]{1,0:T(8,128)(2,1)} fusion(bf16[512,256]{0,1:T(8,128)(2,1)S(1)} %bitcast.20, bf16[256,1024]{1,0:T(8,128)(2,1)S(1)} %all_gather.11), kind=kOutput, calls=%fused_computation.11 | convolution fusion | flops 268959744 | bytes 1835008 | tf_op jit(solution)/shard_map/dot_general | solution.py:76
  75.9 23.9 %reduce-scatter.2.cloned.1.call-done = bf16[512,256]{1,0:T(8,128)(2,1)} async-done(((bf16[512,1024]{1,0:T(8,128)(2,1)}), bf16[512,256]{1,0:T(8,128)(2,1)}) %reduce-scatter.2.cloned.1.call-update) | async-done | bytes 262160 | tf_op jit(solution)/shard_map/reduce_scatter | solution.py:81
  99.8 1.0 add_convert_fusion
  101.0 9.3 %psum.7 = f32[512]{0:T(512)S(1)} all-reduce(f32[512]{0:T(512)S(1)} %fusion.12), channel_id=1, replica_groups=mesh['dp'=8,'mp'=4] {'mp'}, use_global_device_ids=true, to_apply=%region_5.6 | all-reduce | flops 512 | bytes 4096 | tf_op jit(solution)/shard_map/psum | solution.py:86
  110.3 0.8 fusion.14
  (33 shorter events, 4.1 us)
Async XLA Ops:
  7.2 57.7 %all-gather.3.cloned.1.call-start = ((), (), s32[]{:S(2)}) async-start(), calls=%async_computation.1 | async-start | bytes 1310720 | tf_op jit(solution)/shard_map/all_gather | solution.py:62
  7.9 91.9 %reduce-scatter.2.cloned.1.call-start = ((), (), s32[]{:S(2)}) async-start(), calls=%async_computation.2 | async-start | bytes 1310720 | tf_op jit(solution)/shard_map/reduce_scatter | solution.py:81
  7.9 32.3 %collective-permute-start = (bf16[3,128,256]{2,1,0:T(8,128)(2,1)}, bf16[3,128,256]{2,1,0:T(8,128)(2,1)S(1)}, u32[]{:S(2)}, u32[]{:S(2)}) collective-permute-start(bf16[3,128,256]{2,1,0:T(8,128)(2,1)} %param.8), channel_id=1, source_target_pairs={{0,4},{4,8},{8,12},{12,16},{16,20},{20,24},{24,28},{28,0},{1,5},{5... | collective-permute-start | bytes 589832 | tf_op jit(solution)/shard_map/ppermute | solution.py:17
  8.5 32.3 %collective-permute-start.1 = (bf16[3,128,256]{2,1,0:T(8,128)(2,1)}, bf16[3,128,256]{2,1,0:T(8,128)(2,1)S(1)}, u32[]{:S(2)}, u32[]{:S(2)}) collective-permute-start(bf16[3,128,256]{2,1,0:T(8,128)(2,1)} %param.8), channel_id=1, source_target_pairs={{0,28},{4,0},{8,4},{12,8},{16,12},{20,16},{24,20},{28,24},{1,29},{... | collective-permute-start | bytes 589832 | tf_op jit(solution)/shard_map/ppermute | solution.py:20
  25.3 2.9 %copy-start.3 = (bf16[256,128]{1,0:T(8,128)(2,1)S(1)}, bf16[256,128]{1,0:T(8,128)(2,1)}, u32[]{:S(2)}) copy-start(bf16[256,128]{1,0:T(8,128)(2,1)} %param.9) | copy-start | bytes 196612
  40.4 7.1 %collective-permute-start.2 = (bf16[3,128,256]{2,1,0:T(8,128)(2,1)S(1)}, bf16[3,128,256]{2,1,0:T(8,128)(2,1)}, u32[]{:S(2)}, u32[]{:S(2)}) collective-permute-start(bf16[3,128,256]{2,1,0:T(8,128)(2,1)S(1)} %collective-permute-done), channel_id=1, source_target_pairs={{0,4},{4,8},{8,12},{12,16},{16,20},{20,24},{24,28},{28,0},{1,5},{5... | collective-permute-start | bytes 589832 | tf_op jit(solution)/shard_map/ppermute | solution.py:17
  41.0 7.7 %collective-permute-start.3 = (bf16[3,128,256]{2,1,0:T(8,128)(2,1)S(1)}, bf16[3,128,256]{2,1,0:T(8,128)(2,1)}, u32[]{:S(2)}, u32[]{:S(2)}) collective-permute-start(bf16[3,128,256]{2,1,0:T(8,128)(2,1)S(1)} %collective-permute-done.1), channel_id=1, source_target_pairs={{0,28},{4,0},{8,4},{12,8},{16,12},{20,16},{24,20},{28,24},{1,29},{... | collective-permute-start | bytes 589832 | tf_op jit(solution)/shard_map/ppermute | solution.py:20
  48.6 8.1 %collective-permute-start.4 = (bf16[3,128,256]{2,1,0:T(8,128)(2,1)}, bf16[3,128,256]{2,1,0:T(8,128)(2,1)S(1)}, u32[]{:S(2)}, u32[]{:S(2)}) collective-permute-start(bf16[3,128,256]{2,1,0:T(8,128)(2,1)} %collective-permute-done.2), channel_id=1, source_target_pairs={{0,4},{4,8},{8,12},{12,16},{16,20},{20,24},{24,28},{28,0},{1,5},{5... | collective-permute-start | bytes 589832 | tf_op jit(solution)/shard_map/ppermute | solution.py:17
  49.8 8.0 %collective-permute-start.5 = (bf16[3,128,256]{2,1,0:T(8,128)(2,1)}, bf16[3,128,256]{2,1,0:T(8,128)(2,1)S(1)}, u32[]{:S(2)}, u32[]{:S(2)}) collective-permute-start(bf16[3,128,256]{2,1,0:T(8,128)(2,1)} %collective-permute-done.3), channel_id=1, source_target_pairs={{0,28},{4,0},{8,4},{12,8},{16,12},{20,16},{24,20},{28,24},{1,29},{... | collective-permute-start | bytes 589832 | tf_op jit(solution)/shard_map/ppermute | solution.py:20
  56.9 6.2 %collective-permute-start.6 = (bf16[3,128,256]{2,1,0:T(8,128)(2,1)S(1)}, bf16[3,128,256]{2,1,0:T(8,128)(2,1)}, u32[]{:S(2)}, u32[]{:S(2)}) collective-permute-start(bf16[3,128,256]{2,1,0:T(8,128)(2,1)S(1)} %collective-permute-done.4), channel_id=1, source_target_pairs={{0,4},{4,8},{8,12},{12,16},{16,20},{20,24},{24,28},{28,0},{1,5},{5... | collective-permute-start | bytes 589832 | tf_op jit(solution)/shard_map/ppermute | solution.py:17
  69.9 1.5 %copy-start.2 = (bf16[1,512,256]{1,2,0:T(8,128)(2,1)}, bf16[1,512,256]{1,2,0:T(8,128)(2,1)S(1)}, u32[]{:S(2)}) copy-start(bf16[1,512,256]{1,2,0:T(8,128)(2,1)S(1)} %get-tuple-element.11) | copy-start | bytes 786436
  74.3 1.5 %copy-start.4 = (bf16[256]{0:T(256)(128)(2,1)S(1)}, bf16[256]{0:T(256)(128)(2,1)}, u32[]{:S(2)}) copy-start(bf16[256]{0:T(256)(128)(2,1)} %param.11) | copy-start | bytes 1540
  74.4 25.5 %copy-start.1 = (bf16[512,256]{1,0:T(8,128)(2,1)S(1)}, bf16[512,256]{1,0:T(8,128)(2,1)}, u32[]{:S(2)}) copy-start(bf16[512,256]{1,0:T(8,128)(2,1)} %param.6) | copy-start | bytes 786436
  100.8 10.3 %copy-start = (bf16[512,256]{1,0:T(8,128)(2,1)}, bf16[512,256]{1,0:T(8,128)(2,1)S(1)}, u32[]{:S(2)}) copy-start(bf16[512,256]{1,0:T(8,128)(2,1)S(1)} %add_convert_fusion) | copy-start | bytes 786436
Sparse Core Ops, SparseCore 0:
  9.5 32.6 all-gather.2
  76.0 23.8 reduce-scatter.1
